TPU v7x, 128 devices: a whole 4x4x4 slice. The times are simulated.
128 devices in a mesh: req: 2 (over core), seq: 64 (over x, z, y).
Axes of the slice: x: 4, y: 4, z: 4, core: 2. Of those that a mesh axis runs over, the one named last changes fastest.
Arguments:
- image_query: bfloat16 [1024, 1536], P(('req', 'seq')), parts along dimension 0, may hold values from -6 to 6
- image_key: bfloat16 [1024, 1536], P(('req', 'seq')), parts along dimension 0, may hold values from -6 to 6
- image_value: bfloat16 [1024, 1536], P(('req', 'seq')), parts along dimension 0, may hold values from -6 to 6
- text_query: bfloat16 [1024, 1536], P('req'), parts along dimension 0, may hold values from -6 to 6
- text_key: bfloat16 [1024, 1536], P('req'), parts along dimension 0, may hold values from -6 to 6
- text_value: bfloat16 [1024, 1536], P('req'), parts along dimension 0, may hold values from -6 to 6
- image_query_gain: float32 [128], replicated, may hold values from 1 to 8
- image_key_gain: float32 [128], replicated, may hold values from 1 to 8
- text_query_gain: float32 [128], replicated, may hold values from 1 to 2.5
- text_key_gain: float32 [128], replicated, may hold values from 1 to 2.5
- image_order: int32 [1024], P(('req', 'seq')), parts along dimension 0, may hold values from 0 to 511, each once
- text_length: int32 [2], P('req'), parts along dimension 0, may hold values from 256 to 512
Outputs:
- image_out: bfloat16 [1024, 1536], P(('req', 'seq')), parts along dimension 0
- text_out: bfloat16 [1024, 1536], P(('req', 'seq')), parts along dimension 0
There are 2 independent parts, one for each index of `req`. A program takes and returns all parts, laid end to end along the dimension named above; an argument that names none is the same for every part. Nothing has to cross between parts.
Inputs may be any that keep to these rules, and one draw needn't show every extreme that they name: `image_order`: every position 0 to 511 appears once.
All inputs are finite; a program needn't handle non-finite values.
Results may differ from a plain program's by a relative error of at most 0.005.
The roundings to bfloat16 on the way count: a program that leaves them out, or rounds other values in their place, can miss the bound.
Values may be sent and summed in bfloat16 or wider, within the bound.
No kernel may reach another device: no remote copies, remote signals or barrier semaphores. Data moves between devices by JAX's collectives and lax.ppermute only.
A program may use at most 64 MiB of HBM per device.

v0:
```python
import jax
import jax.numpy as jnp
import numpy as np
from jax import lax
from jax.experimental import pallas as pl
from jax.experimental.pallas import tpu as pltpu
from jax.sharding import PartitionSpec as P

HD = 128
GRID_W = 64
SIDE = 4
EPS = 1e-06
MASKED = -1e30
SCALE = HD ** (-0.5)
LOG2E = 1.4426950408889634

VM = pl.BlockSpec(memory_space=pltpu.VMEM)
SM = pl.BlockSpec(memory_space=pltpu.SMEM)
HB = pl.BlockSpec(memory_space=pltpu.HBM)


def split_index(i):
    return i // (SIDE * SIDE), (i // SIDE) % SIDE, i % SIDE


def parity(i):
    return (i ^ (i >> 1)) & 1


def head_group(z, y):
    return parity(z) * 2 + parity(y)


def key_group(x, z):
    return parity(x) * 2 + (z >> 1)


def member(x, z, y):
    return parity(x) * 8 + z * 2 + parity(y)


HEAD_STEPS = ((0, 0, 0), (0, 1, 1), (0, 1, 0), (0, 0, 1))
QUERY_STEPS = ((0, 0, 0), (0, 3, 0), (1, 0, 0), (1, 3, 0))
KEY_STEPS = ((0, 0, 0), (3, 0, 3), (3, 0, 0), (0, 0, 3))


def query_groups():
    groups = {}
    for i in range(SIDE**3):
        x, z, y = split_index(i)
        groups.setdefault((x >> 1, y >> 1), {})[member(x, z, y)] = i
    return [[g[j] for j in range(len(g))] for g in groups.values()]


def exchange(value, step):
    pairs = []
    for i in range(SIDE**3):
        x, z, y = split_index(i)
        pairs.append((i, ((x ^ step[0]) * SIDE + (z ^ step[1])) * SIDE + (y ^ step[2])))
    return in_vmem(lax.ppermute(value, "seq", pairs))


def in_vmem(value):
    return pltpu.with_memory_space_constraint(value, pltpu.VMEM)


def vmem_call(kernel, **options):
    call = pl.pallas_call(kernel, **options)
    return lambda *args: jax.tree.map(in_vmem, call(*args))


def head_norm(x, gain):
    mean_square = jnp.mean(x * x, axis=-1, keepdims=True)
    return x * lax.rsqrt(mean_square + EPS) * gain


def frequencies():
    pair = np.arange(HD) // 2
    within = np.where(pair < 8, pair, np.where(pair < 36, pair - 8, pair - 36)).astype(np.float64)
    dim = np.where(pair < 8, 16.0, 56.0)
    return (10000.0 ** (-2.0 * within / dim)).astype(np.float32).reshape(1, HD)


def load(pairs, sems):
    copies = [pltpu.make_async_copy(src, dst, sems.at[i]) for i, (src, dst) in enumerate(pairs)]
    for c in copies:
        c.start()
    for c in copies:
        c.wait()


def prep_kernel(heads, half, order_h, freq_h, q_h, k_h, v_h, qg_h, kg_h, o0, o1, o2, o3, order, freq, q_in, k_in, v_in, qg, kg, q_s, k_s, sems):
    load(
        ((order_h, order), (freq_h, freq), (q_h, q_in), (k_h, k_in), (v_h, v_in), (qg_h, qg), (kg_h, kg)),
        sems,
    )
    rows = q_in.shape[0]
    lane = lax.broadcasted_iota(jnp.int32, (rows, HD), 1)
    row = lax.broadcasted_iota(jnp.int32, (rows, HD), 0)
    position = jnp.zeros((rows, HD), jnp.int32)
    for i in range(rows):
        position = jnp.where(row == i, order[i], position)
    inside = position & (half - 1)
    pair = lane >> 1
    coordinate = jnp.where(
        pair < 8,
        position >> (half.bit_length() - 1),
        jnp.where(pair < 36, inside >> (GRID_W.bit_length() - 1), inside & (GRID_W - 1)),
    )
    angle = coordinate.astype(jnp.float32) * freq[...]
    cosine = jnp.cos(angle)
    sine = jnp.sin(angle)
    even = (lane & 1) == 0
    sine = jnp.where(even, -sine, sine)
    blocks = [
        src[:, h * HD : (h + 1) * HD].astype(jnp.float32) for src in (q_in, k_in) for h in range(heads)
    ]
    whole = jnp.concatenate(blocks, axis=0)
    mean_square = jnp.mean(whole * whole, axis=-1, keepdims=True)
    whole = whole * lax.rsqrt(mean_square + EPS)
    for n in range(2 * heads):
        gain, dst, h = (qg, q_s, n) if n < heads else (kg, k_s, n - heads)
        x = whole[n * rows : (n + 1) * rows] * gain[...]
        partner = jnp.where(even, pltpu.roll(x, HD - 1, 1), pltpu.roll(x, 1, 1))
        dst[:, h * HD : (h + 1) * HD] = (x * cosine + partner * sine).astype(jnp.bfloat16)
    width = heads // SIDE * HD
    _, z, y = split_index(lax.axis_index("seq"))
    for step, out in zip(HEAD_STEPS, (o0, o1, o2, o3)):
        start = pl.multiple_of(head_group(z ^ step[1], y ^ step[2]) * width, HD)
        out[:, 0:width] = k_s[:, pl.ds(start, width)]
        out[:, width : 2 * width] = v_in[:, pl.ds(start, width)]
        out[:, 2 * width : 3 * width] = q_s[:, pl.ds(start, width)]


def pack_kernel(a0, a1, a2, a3, order_only, kv, q):
    rows = a0.shape[0]
    width = q.shape[1]
    for j, a in enumerate((a0, a1, a2, a3)):
        kv[j * rows : (j + 1) * rows, :] = a[:, : 2 * width]
        q[j * rows : (j + 1) * rows, :] = a[:, 2 * width :]


def join_kernel(a, b, out):
    rows = a.shape[0]
    out[:rows, :] = a[...]
    out[rows:, :] = b[...]


def text_kernel(q_h, k_h, v_h, qg_h, kg_h, length_h, q_out, k_out, v_out, bias, length, q_in, k_in, qg, kg, sems):
    block, width = k_in.shape
    x, z, y = split_index(lax.axis_index("seq"))
    group = key_group(x, z)
    cols = pl.ds(pl.multiple_of(head_group(z, y) * width, HD), width)
    k_rows = pl.ds(pl.multiple_of(group * block, block), block)
    pieces = [
        (length_h, length),
        (k_h.at[k_rows, cols], k_in),
        (v_h.at[k_rows, cols], v_out),
        (qg_h, qg),
        (kg_h, kg),
    ]
    own = q_in.shape[1]
    for j in range(q_in.shape[0]):
        px, jz, py = j >> 3, (j >> 1) & 3, j & 1
        jx = (x & 2) + (px ^ (x >> 1))
        jy = (y & 2) + (py ^ (y >> 1))
        start = ((jx * SIDE + jz) * SIDE + jy) * own
        pieces.append((q_h.at[pl.ds(pl.multiple_of(start, own), own), cols], q_in.at[j]))
    load(pieces, sems)
    for gain, dst in ((qg, q_out), (kg, k_out)):
        g = gain[...]
        for h in range(width // HD):
            at = slice(h * HD, (h + 1) * HD)
            if dst is q_out:
                rows = q_in[:, :, at].astype(jnp.float32).reshape(block, HD)
            else:
                rows = k_in[:, at].astype(jnp.float32)
            dst[:, at] = head_norm(rows, g).astype(jnp.bfloat16)
    key = lax.broadcasted_iota(jnp.int32, bias.shape, 1) + group * block
    bias[...] = jnp.where(key < length[0], 0.0, MASKED)


def attend_kernel(kv0, kv1, kv2, kv3, q0, q1, qt, kt, vt, bias, out):
    kvs, qs = (kv0, kv1, kv2, kv3), (q0, q1)
    width = qt.shape[1]
    heads = width // HD
    text_keys = kt.shape[0]
    image_rows = 2 * q0.shape[0]
    rows = image_rows + qt.shape[0]
    x, z, y = split_index(lax.axis_index("seq"))
    masked = bias[0:1, :]
    lane = lax.broadcasted_iota(jnp.int32, (rows, HD), 1)
    stats = jnp.zeros((rows, HD), jnp.float32)
    blended = []
    for h in range(heads):
        cols = slice(h * HD, (h + 1) * HD)
        vcols = slice(width + h * HD, width + (h + 1) * HD)
        query = jnp.concatenate([r[:, cols] for r in qs] + [qt[:, cols]], axis=0)
        key = jnp.concatenate([kt[:, cols]] + [r[:, cols] for r in kvs], axis=0)
        value = jnp.concatenate([vt[:, cols]] + [r[:, vcols] for r in kvs], axis=0)
        s = lax.dot_general(query, key, (((1,), (1,)), ((), ())), preferred_element_type=jnp.float32)
        s = jnp.concatenate([s[:, :text_keys] + masked, s[:, text_keys:]], axis=1)
        m = jnp.max(s, axis=1, keepdims=True)
        e = jnp.exp2((s - m) * (SCALE * LOG2E))
        m = m * SCALE
        l = jnp.sum(e, axis=1, keepdims=True)
        blended.append(jnp.dot(e.astype(jnp.bfloat16), value, preferred_element_type=jnp.float32))
        for first, value in ((h, m), (24 + h, l)):
            for piece in range(3 if first == h else 2):
                stats = jnp.where(lane == first + 8 * piece, value, stats)
                value = value - value.astype(jnp.bfloat16).astype(jnp.float32)
    blended.append(stats)
    for a, key_step in enumerate(QUERY_STEPS):
        for b, head_step in enumerate(HEAD_STEPS):
            i = a * SIDE + b
            there = member(x ^ key_step[0], z ^ key_step[1] ^ head_step[1], y ^ head_step[2])
            for c, part in enumerate(blended):
                cols = slice(c * HD, (c + 1) * HD)
                out[there, 0:8, cols] = part[i * 8 : (i + 1) * 8].astype(jnp.bfloat16)
                begin = image_rows + i * 8
                out[i, 8:16, cols] = part[begin : begin + 8].astype(jnp.bfloat16)


def combine_kernel(got, image_out, text_out):
    heads = (got.shape[2] - HD) // HD
    width = heads * HD
    half = image_out.shape[0]
    members = [[None] * SIDE for _ in range(SIDE)]
    for j in range(got.shape[0]):
        px, z, py = j >> 3, (j >> 1) & 3, j & 1
        members[px * 2 + (z >> 1)][parity(z) * 2 + py] = j

    def stacked(key, cols):
        return jnp.concatenate([got[m, :, cols].astype(jnp.float32) for m in members[key]], axis=0)

    stats = [stacked(key, slice(width, width + HD)) for key in range(SIDE)]
    peaks = [s + pltpu.roll(s, HD - 8, 1) + pltpu.roll(s, HD - 16, 1) for s in stats]
    sums = [pltpu.roll(s, HD - 24, 1) + pltpu.roll(s, HD - 32, 1) for s in stats]
    top = jnp.maximum(jnp.maximum(peaks[0], peaks[1]), jnp.maximum(peaks[2], peaks[3]))
    factors = [jnp.exp(p - top) for p in peaks]
    total = factors[0] * sums[0] + factors[1] * sums[1] + factors[2] * sums[2] + factors[3] * sums[3]
    lane = lax.broadcasted_iota(jnp.int32, total.shape, 1)
    inverse = 1.0 / jnp.where(lane < heads, total, 1.0)
    weights = [f * inverse for f in factors]
    for h in range(heads):
        acc = 0.0
        for key in range(SIDE):
            acc = acc + stacked(key, slice(h * HD, (h + 1) * HD)) * weights[key][:, h : h + 1]
        for g in range(SIDE):
            cols = slice(g * width + h * HD, g * width + (h + 1) * HD)
            rows = acc[g * 2 * half : (g + 1) * 2 * half].astype(jnp.bfloat16)
            image_out[:, cols] = rows[:half]
            text_out[:, cols] = rows[half:]


def local(
    image_query,
    image_key,
    image_value,
    text_query,
    text_key,
    text_value,
    image_query_gain,
    image_key_gain,
    text_query_gain,
    text_key_gain,
    image_order,
    text_length,
):
    rows, model = image_query.shape
    heads = model // HD
    width = model // SIDE
    text_rows = text_query.shape[0]
    block = text_rows // SIDE
    parts = SIDE * SIDE
    half = rows * SIDE**3 // 2
    bf, f32 = jnp.bfloat16, jnp.float32
    struct = jax.ShapeDtypeStruct
    gains = [g.reshape(1, HD) for g in (image_query_gain, image_key_gain, text_query_gain, text_key_gain)]

    own = vmem_call(
        lambda *refs: prep_kernel(heads, half, *refs),
        out_shape=[pltpu.VMEM((rows, 3 * width), bf)] * SIDE,
        in_specs=[HB] * 7,
        out_specs=[VM] * SIDE,
        scratch_shapes=[
            pltpu.SMEM((rows,), jnp.int32),
            pltpu.VMEM((1, HD), f32),
            pltpu.VMEM((rows, model), bf),
            pltpu.VMEM((rows, model), bf),
            pltpu.VMEM((rows, model), bf),
            pltpu.VMEM((1, HD), f32),
            pltpu.VMEM((1, HD), f32),
            pltpu.VMEM((rows, model), bf),
            pltpu.VMEM((rows, model), bf),
            pltpu.SemaphoreType.DMA((7,)),
        ],
        name="prep",
    )(image_order, jnp.asarray(frequencies()), image_query, image_key, image_value, gains[0], gains[1])

    from_y = [own[0]] + [exchange(own[d], HEAD_STEPS[d]) for d in range(1, SIDE)]

    qt, kt, vt, bias = vmem_call(
        text_kernel,
        out_shape=[pltpu.VMEM((block, width), bf)] * 3 + [pltpu.VMEM((8, block), f32)],
        in_specs=[HB] * 6,
        out_specs=[VM] * 4,
        scratch_shapes=[
            pltpu.SMEM((1,), jnp.int32),
            pltpu.VMEM((parts, block // parts, width), bf),
            pltpu.VMEM((block, width), bf),
            pltpu.VMEM((1, HD), f32),
            pltpu.VMEM((1, HD), f32),
            pltpu.SemaphoreType.DMA((5 + parts,)),
        ],
        cost_estimate=pl.CostEstimate(flops=20_000_000, bytes_accessed=600_000, transcendentals=0),
        name="text",
    )(text_query, text_key, text_value, gains[2], gains[3], text_length)

    kv, q = vmem_call(
        pack_kernel,
        out_shape=[pltpu.VMEM((SIDE * rows, 2 * width), bf), pltpu.VMEM((SIDE * rows, width), bf)],
        in_specs=[VM] * SIDE + [VM],
        out_specs=[VM] * 2,
        name="pack",
    )(*from_y, bias)

    q_next = exchange(q, QUERY_STEPS[1])
    kvs = [kv]
    for i in range(1, SIDE):
        kvs.append(exchange(kv, KEY_STEPS[i]))
    q_two = vmem_call(
        join_kernel,
        out_shape=pltpu.VMEM((2 * SIDE * rows, width), bf),
        in_specs=[VM] * 2,
        out_specs=VM,
        name="join",
    )(q, q_next)
    q_last = exchange(q_two, QUERY_STEPS[2])

    out_rows = rows + text_rows // SIDE**3
    partial = pl.pallas_call(
        attend_kernel,
        out_shape=pltpu.VMEM((parts, out_rows, width + HD), bf),
        in_specs=[VM] * 10,
        out_specs=VM,
        name="attend",
    )(*kvs, q_two, q_last, qt, kt, vt, bias)

    got = in_vmem(lax.all_to_all(partial, "seq", 0, 0, axis_index_groups=query_groups(), tiled=True))

    return pl.pallas_call(
        combine_kernel,
        out_shape=[struct((rows, model), bf), struct((out_rows - rows, model), bf)],
        in_specs=[VM],
        out_specs=[VM] * 2,
        name="combine",
    )(got)


def whole(*args):
    return tuple(local(*args))


def solution(mesh):
    token = P(("req", "seq"), None)
    text = P("req", None)
    return jax.shard_map(
        whole,
        mesh=mesh,
        in_specs=(token, token, token, text, text, text, P(), P(), P(), P(), P(("req", "seq")), P("req")),
        out_specs=(token, token),
        check_vma=False,
    )
```

profile of v0, /device:TPU:0, one launch (start us, length us, event | category | flops | bytes accessed | tf_op | source)
XLA Modules:
  0.0 37.3 jit_solution(5714957928891196511)
XLA Ops:
  0.6 1.1 %prep.1 = (bf16[8,1152]{1,0:T(8,128)(2,1)S(1)}, bf16[8,1152]{1,0:T(8,128)(2,1)S(1)}, bf16[8,1152]{1,0:T(8,128)(2,1)S(1)}, bf16[8,1152]{1,0:T(8,128)(2,1)S(1)}) custom-call(s32[8]{0:T(128)} %refs_0_.1, f32[1,128]{1,0:T(1,128)} %constant.2.clone.refs_1_, bf16[8,1536]{1,0:T(8,128)(2,1)} %refs_2_.1, bf16[8,1536]{1,0:T(8,128)(2,1)} %refs_3_.1, ...), custom_call_target="tpu_custom_call" | custom-call | tf_op jit(solution)/shard_map/prep/pallas_call | solution.py:69
  1.7 3.1 %collective-permute-start = (bf16[8,1152]{1,0:T(8,128)(2,1)S(1)}, bf16[8,1152]{1,0:T(8,128)(2,1)S(1)}, u32[]{:S(2)}, u32[]{:S(2)}) collective-permute-start(bf16[8,1152]{1,0:T(8,128)(2,1)S(1)} %get-tuple-element.13), channel_id=1, source_target_pairs={{0,5},{1,4},{2,7},{3,6},{4,1},{5,0},{6,3},{7,2},{8,13},{9,12},{10,... | collective-permute-start | bytes 55304 | tf_op jit(solution)/shard_map/ppermute | solution.py:60
  4.8 0.1 collective-permute-start.1
  4.9 0.5 %collective-permute-start.2 = (bf16[8,1152]{1,0:T(8,128)(2,1)S(1)}, bf16[8,1152]{1,0:T(8,128)(2,1)S(1)}, u32[]{:S(2)}, u32[]{:S(2)}) collective-permute-start(bf16[8,1152]{1,0:T(8,128)(2,1)S(1)} %get-tuple-element.15), channel_id=1, source_target_pairs={{0,1},{1,0},{2,3},{3,2},{4,5},{5,4},{6,7},{7,6},{8,9},{9,8},{10,11... | collective-permute-start | bytes 55304 | tf_op jit(solution)/shard_map/ppermute | solution.py:60
  6.1 1.4 %text.1 = (bf16[128,384]{1,0:T(8,128)(2,1)S(1)}, bf16[128,384]{1,0:T(8,128)(2,1)S(1)}, bf16[128,384]{1,0:T(8,128)(2,1)S(1)}, f32[8,128]{1,0:T(8,128)S(1)}) custom-call(bf16[512,1536]{1,0:T(8,128)(2,1)} %q_h.1, bf16[512,1536]{1,0:T(8,128)(2,1)} %k_h.1, bf16[512,1536]{1,0:T(8,128)(2,1)} %v_h.1, f32[1,128]{1,0:T(1,128)} %bitcast.6, f32[1,128]{1,0:T(1,128)} %bitcast.7, ...), custom_call_target="tpu_custom_call" | custom-call | flops 20000000 | bytes 600000 | tf_op jit(solution)/shard_map/text/pallas_call | solution.py:69
  7.5 0.0 collective-permute-done.a1
  7.5 1.1 %collective-permute-done.1.a2 = bf16[8,1152]{1,0:T(8,128)(2,1)S(1)} collective-permute-done((bf16[8,1152]{1,0:T(8,128)(2,1)S(1)}, bf16[8,1152]{1,0:T(8,128)(2,1)S(1)}, u32[]{:S(2)}, u32[]{:S(2)}) %collective-permute-start.1) | collective-permute-done | bytes 18464 | tf_op jit(solution)/shard_map/ppermute | solution.py:60
  8.6 0.1 collective-permute-done.2.a3
  8.7 4.0 %collective-permute-start.6 = (bf16[32,384]{1,0:T(8,128)(2,1)S(1)}, bf16[32,384]{1,0:T(8,128)(2,1)S(1)}, u32[]{:S(2)}, u32[]{:S(2)}) collective-permute-start(bf16[32,384]{1,0:T(8,128)(2,1)S(1)} %get-tuple-element.18.a), channel_id=1, source_target_pairs={{0,12},{1,13},{2,14},{3,15},{4,8},{5,9},{6,10},{7,11},{8,4},{9,5},... | collective-permute-start | bytes 73736 | tf_op jit(solution)/shard_map/ppermute | solution.py:60
  12.8 2.2 %collective-permute-start.5 = (bf16[32,768]{1,0:T(8,128)(2,1)S(1)}, bf16[32,768]{1,0:T(8,128)(2,1)S(1)}, u32[]{:S(2)}, u32[]{:S(2)}) collective-permute-start(bf16[32,768]{1,0:T(8,128)(2,1)S(1)} %get-tuple-element.17.kv0), channel_id=1, source_target_pairs={{0,3},{1,2},{2,1},{3,0},{4,7},{5,6},{6,5},{7,4},{8,11},{9,10},{10,... | collective-permute-start | bytes 147464 | tf_op jit(solution)/shard_map/ppermute | solution.py:60
  14.9 2.8 %collective-permute-start.4 = (bf16[32,768]{1,0:T(8,128)(2,1)S(1)}, bf16[32,768]{1,0:T(8,128)(2,1)S(1)}, u32[]{:S(2)}, u32[]{:S(2)}) collective-permute-start(bf16[32,768]{1,0:T(8,128)(2,1)S(1)} %get-tuple-element.17.kv0), channel_id=1, source_target_pairs={{0,48},{1,49},{2,50},{3,51},{4,52},{5,53},{6,54},{7,55},{8,56},{9,... | collective-permute-start | bytes 147464 | tf_op jit(solution)/shard_map/ppermute | solution.py:60
  17.7 1.0 %collective-permute-start.3 = (bf16[32,768]{1,0:T(8,128)(2,1)S(1)}, bf16[32,768]{1,0:T(8,128)(2,1)S(1)}, u32[]{:S(2)}, u32[]{:S(2)}) collective-permute-start(bf16[32,768]{1,0:T(8,128)(2,1)S(1)} %get-tuple-element.17.kv0), channel_id=1, source_target_pairs={{0,51},{1,50},{2,49},{3,48},{4,55},{5,54},{6,53},{7,52},{8,59},{9,... | collective-permute-start | bytes 147464 | tf_op jit(solution)/shard_map/ppermute | solution.py:60
  18.7 0.0 collective-permute-done.6.b
  18.7 0.4 collective-permute-start.7
  19.0 0.0 collective-permute-done.5.kv3
  19.0 1.6 %collective-permute-done.4.kv2 = bf16[32,768]{1,0:T(8,128)(2,1)S(1)} collective-permute-done((bf16[32,768]{1,0:T(8,128)(2,1)S(1)}, bf16[32,768]{1,0:T(8,128)(2,1)S(1)}, u32[]{:S(2)}, u32[]{:S(2)}) %collective-permute-start.4) | collective-permute-done | bytes 49184 | tf_op jit(solution)/shard_map/ppermute | solution.py:60
  20.6 4.5 %collective-permute-done.3.kv1 = bf16[32,768]{1,0:T(8,128)(2,1)S(1)} collective-permute-done((bf16[32,768]{1,0:T(8,128)(2,1)S(1)}, bf16[32,768]{1,0:T(8,128)(2,1)S(1)}, u32[]{:S(2)}, u32[]{:S(2)}) %collective-permute-start.3) | collective-permute-done | bytes 49184 | tf_op jit(solution)/shard_map/ppermute | solution.py:60
  25.1 0.0 collective-permute-done.7.q1
  25.1 0.8 %attend.1 = bf16[16,16,512]{2,1,0:T(8,128)(2,1)S(1)} custom-call(bf16[32,768]{1,0:T(8,128)(2,1)S(1)} %get-tuple-element.17.kv0, bf16[32,768]{1,0:T(8,128)(2,1)S(1)} %collective-permute-done.3.kv1, bf16[32,768]{1,0:T(8,128)(2,1)S(1)} %collective-permute-done.4.kv2, bf16[32,768]{1,0:T(8,128)(2,1)S(1)} %collective-permute-done.5.kv3, ...), custom_call_target="tpu_custom_call" | custom-call | tf_op jit(solution)/shard_map/attend/pallas_call | solution.py:342
  25.9 10.4 %all_to_all.5.got = bf16[16,16,512]{2,1,0:T(8,128)(2,1)S(1)} all-to-all(bf16[16,16,512]{2,1,0:T(8,128)(2,1)S(1)} %attend.1), channel_id=1, replica_groups={{0,1,4,5,8,9,12,13,16,17,20,21,24,25,28,29},{3,2,7,6,11,10,15,14,19,18,..., dimensions={0} | all-to-all | bytes 524288 | tf_op jit(solution)/shard_map/all_to_all | solution.py:350
  36.4 0.9 %combine.1 = (bf16[8,1536]{1,0:T(8,128)(2,1)}, bf16[8,1536]{1,0:T(8,128)(2,1)}) custom-call(bf16[16,16,512]{2,1,0:T(8,128)(2,1)S(1)} %all_to_all.5.got), custom_call_target="tpu_custom_call" | custom-call | tf_op jit(solution)/shard_map/combine/pallas_call | solution.py:352
  (2 shorter events, 0.0 us)
Async XLA Ops:
  1.7 5.8 %collective-permute-start = (bf16[8,1152]{1,0:T(8,128)(2,1)S(1)}, bf16[8,1152]{1,0:T(8,128)(2,1)S(1)}, u32[]{:S(2)}, u32[]{:S(2)}) collective-permute-start(bf16[8,1152]{1,0:T(8,128)(2,1)S(1)} %get-tuple-element.13), channel_id=1, source_target_pairs={{0,5},{1,4},{2,7},{3,6},{4,1},{5,0},{6,3},{7,2},{8,13},{9,12},{10,... | collective-permute-start | bytes 55304 | tf_op jit(solution)/shard_map/ppermute | solution.py:60
  4.8 3.8 %collective-permute-start.1 = (bf16[8,1152]{1,0:T(8,128)(2,1)S(1)}, bf16[8,1152]{1,0:T(8,128)(2,1)S(1)}, u32[]{:S(2)}, u32[]{:S(2)}) collective-permute-start(bf16[8,1152]{1,0:T(8,128)(2,1)S(1)} %get-tuple-element.14), channel_id=1, source_target_pairs={{0,4},{1,5},{2,6},{3,7},{4,0},{5,1},{6,2},{7,3},{8,12},{9,13},{10,... | collective-permute-start | bytes 55304 | tf_op jit(solution)/shard_map/ppermute | solution.py:60
  4.9 3.8 %collective-permute-start.2 = (bf16[8,1152]{1,0:T(8,128)(2,1)S(1)}, bf16[8,1152]{1,0:T(8,128)(2,1)S(1)}, u32[]{:S(2)}, u32[]{:S(2)}) collective-permute-start(bf16[8,1152]{1,0:T(8,128)(2,1)S(1)} %get-tuple-element.15), channel_id=1, source_target_pairs={{0,1},{1,0},{2,3},{3,2},{4,5},{5,4},{6,7},{7,6},{8,9},{9,8},{10,11... | collective-permute-start | bytes 55304 | tf_op jit(solution)/shard_map/ppermute | solution.py:60
  8.7 10.0 %collective-permute-start.6 = (bf16[32,384]{1,0:T(8,128)(2,1)S(1)}, bf16[32,384]{1,0:T(8,128)(2,1)S(1)}, u32[]{:S(2)}, u32[]{:S(2)}) collective-permute-start(bf16[32,384]{1,0:T(8,128)(2,1)S(1)} %get-tuple-element.18.a), channel_id=1, source_target_pairs={{0,12},{1,13},{2,14},{3,15},{4,8},{5,9},{6,10},{7,11},{8,4},{9,5},... | collective-permute-start | bytes 73736 | tf_op jit(solution)/shard_map/ppermute | solution.py:60
  12.8 6.3 %collective-permute-start.5 = (bf16[32,768]{1,0:T(8,128)(2,1)S(1)}, bf16[32,768]{1,0:T(8,128)(2,1)S(1)}, u32[]{:S(2)}, u32[]{:S(2)}) collective-permute-start(bf16[32,768]{1,0:T(8,128)(2,1)S(1)} %get-tuple-element.17.kv0), channel_id=1, source_target_pairs={{0,3},{1,2},{2,1},{3,0},{4,7},{5,6},{6,5},{7,4},{8,11},{9,10},{10,... | collective-permute-start | bytes 147464 | tf_op jit(solution)/shard_map/ppermute | solution.py:60
  14.9 5.7 %collective-permute-start.4 = (bf16[32,768]{1,0:T(8,128)(2,1)S(1)}, bf16[32,768]{1,0:T(8,128)(2,1)S(1)}, u32[]{:S(2)}, u32[]{:S(2)}) collective-permute-start(bf16[32,768]{1,0:T(8,128)(2,1)S(1)} %get-tuple-element.17.kv0), channel_id=1, source_target_pairs={{0,48},{1,49},{2,50},{3,51},{4,52},{5,53},{6,54},{7,55},{8,56},{9,... | collective-permute-start | bytes 147464 | tf_op jit(solution)/shard_map/ppermute | solution.py:60
  17.7 7.4 %collective-permute-start.3 = (bf16[32,768]{1,0:T(8,128)(2,1)S(1)}, bf16[32,768]{1,0:T(8,128)(2,1)S(1)}, u32[]{:S(2)}, u32[]{:S(2)}) collective-permute-start(bf16[32,768]{1,0:T(8,128)(2,1)S(1)} %get-tuple-element.17.kv0), channel_id=1, source_target_pairs={{0,51},{1,50},{2,49},{3,48},{4,55},{5,54},{6,53},{7,52},{8,59},{9,... | collective-permute-start | bytes 147464 | tf_op jit(solution)/shard_map/ppermute | solution.py:60
  18.7 6.4 %collective-permute-start.7 = (bf16[64,384]{1,0:T(8,128)(2,1)S(1)}, bf16[64,384]{1,0:T(8,128)(2,1)S(1)}, u32[]{:S(2)}, u32[]{:S(2)}) collective-permute-start(bf16[64,384]{1,0:T(8,128)(2,1)S(1)} %join.1.q0), channel_id=1, source_target_pairs={{0,16},{1,17},{2,18},{3,19},{4,20},{5,21},{6,22},{7,23},{8,24},{9,... | collective-permute-start | bytes 147464 | tf_op jit(solution)/shard_map/ppermute | solution.py:60
where the time goes:
time: 37.6 us; the launch traced here: 37.3 us
  starting transfers between devices  14.1 us (38%)
  blocking collectives  10.4 us (28%)
  waiting for transfers between devices  7.24 us (19%)
  Pallas kernels  4.23 us (11%)
  between operations  1.33 us (4%)
    ppermute x8, starting transfers between devices, exchange(): return in_vmem(lax.ppermute(value, 'seq', pairs))  14.1 us
    all_to_all x1, blocking collectives, local(): lax.all_to_all(partial, 'seq', 0, 0, axis_index_groups=query_groups(), ti...  10.4 us
    ppermute x8, waiting for transfers between devices, exchange(): return in_vmem(lax.ppermute(value, 'seq', pairs))  7.24 us
    pallas_call x4, Pallas kernels, vmem_call(): return lambda *args: jax.tree.map(in_vmem, call(*args))  2.46 us
    pallas_call x1, Pallas kernels, local(): pl.pallas_call(combine_kernel, out_shape=[struct((rows, model), bf), stru...  0.94 us
    pallas_call x1, Pallas kernels, local(): pl.pallas_call(attend_kernel, out_shape=pltpu.VMEM((parts, out_rows, widt...  0.83 us
  transfers between devices with their start and end apart: 8, of which 4 were waited for; matrix products, arithmetic and copies ran while one was open for 0% of the time, Pallas kernels for 4%

commit v1 on v0

--- a/solution.py
+++ b/solution.py
@@ -19,8 +19,19 @@
 HB = pl.BlockSpec(memory_space=pltpu.HBM)
 
 
+ROLES = (1, 2, 0)
+
+
 def split_index(i):
-    return i // (SIDE * SIDE), (i // SIDE) % SIDE, i % SIDE
+    raw = (i // (SIDE * SIDE), (i // SIDE) % SIDE, i % SIDE)
+    return tuple(raw[r] for r in ROLES)
+
+
+def join_index(x, z, y):
+    raw = [None] * 3
+    for r, c in zip(ROLES, (x, z, y)):
+        raw[r] = c
+    return (raw[0] * SIDE + raw[1]) * SIDE + raw[2]
 
 
 def parity(i):
@@ -36,7 +47,7 @@
 
 
 def member(x, z, y):
-    return parity(x) * 8 + z * 2 + parity(y)
+    return parity(x) * 8 + z * 2 + (parity(y) ^ 1)
 
 
 HEAD_STEPS = ((0, 0, 0), (0, 1, 1), (0, 1, 0), (0, 0, 1))
@@ -56,7 +67,7 @@
     pairs = []
     for i in range(SIDE**3):
         x, z, y = split_index(i)
-        pairs.append((i, ((x ^ step[0]) * SIDE + (z ^ step[1])) * SIDE + (y ^ step[2])))
+        pairs.append((i, join_index(x ^ step[0], z ^ step[1], y ^ step[2])))
     return in_vmem(lax.ppermute(value, "seq", pairs))
 
 
@@ -161,10 +172,10 @@
     ]
     own = q_in.shape[1]
     for j in range(q_in.shape[0]):
-        px, jz, py = j >> 3, (j >> 1) & 3, j & 1
+        px, jz, py = j >> 3, (j >> 1) & 3, (j & 1) ^ 1
         jx = (x & 2) + (px ^ (x >> 1))
         jy = (y & 2) + (py ^ (y >> 1))
-        start = ((jx * SIDE + jz) * SIDE + jy) * own
+        start = join_index(jx, jz, jy) * own
         pieces.append((q_h.at[pl.ds(pl.multiple_of(start, own), own), cols], q_in.at[j]))
     load(pieces, sems)
     for gain, dst in ((qg, q_out), (kg, k_out)):
@@ -227,7 +238,7 @@
     half = image_out.shape[0]
     members = [[None] * SIDE for _ in range(SIDE)]
     for j in range(got.shape[0]):
-        px, z, py = j >> 3, (j >> 1) & 3, j & 1
+        px, z, py = j >> 3, (j >> 1) & 3, (j & 1) ^ 1
         members[px * 2 + (z >> 1)][parity(z) * 2 + py] = j
 
     def stacked(key, cols):

time: 37.6 us -> 36.6 us (0.973)
  blocking collectives: 10.4 us -> 9.42 us
  waiting for transfers between devices: 7.24 us -> 8.01 us
  starting transfers between devices: 14.1 us -> 13.4 us
    all_to_all x1, blocking collectives: 10.4 us -> 9.42 us  [local(): lax.all_to_all(partial, 'seq', 0, 0, axis_index_groups=query_groups(), ti...]
    ppermute x8, waiting for transfers between devices: 7.24 us -> 8.01 us  [exchange(): return in_vmem(lax.ppermute(value, 'seq', pairs))]
    ppermute x8, starting transfers between devices: 14.1 us -> 13.4 us  [exchange(): return in_vmem(lax.ppermute(value, 'seq', pairs))]
where the time goes in v1:
time: 36.6 us; the launch traced here: 36.4 us
  starting transfers between devices  13.4 us (37%)
  blocking collectives  9.42 us (26%)
  waiting for transfers between devices  8.01 us (22%)
  Pallas kernels  4.23 us (12%)
  between operations  1.34 us (4%)
    ppermute x8, starting transfers between devices, exchange(): return in_vmem(lax.ppermute(value, 'seq', pairs))  13.4 us
    all_to_all x1, blocking collectives, local(): lax.all_to_all(partial, 'seq', 0, 0, axis_index_groups=query_groups(), ti...  9.42 us
    ppermute x8, waiting for transfers between devices, exchange(): return in_vmem(lax.ppermute(value, 'seq', pairs))  8.01 us
    pallas_call x4, Pallas kernels, vmem_call(): return lambda *args: jax.tree.map(in_vmem, call(*args))  2.47 us
    pallas_call x1, Pallas kernels, local(): pl.pallas_call(combine_kernel, out_shape=[struct((rows, model), bf), stru...  0.94 us
    pallas_call x1, Pallas kernels, local(): pl.pallas_call(attend_kernel, out_shape=pltpu.VMEM((parts, out_rows, widt...  0.83 us
  transfers between devices with their start and end apart: 8, of which 4 were waited for; matrix products, arithmetic and copies ran while one was open for 0% of the time, Pallas kernels for 4%

profile of v1, /device:TPU:0, one launch (start us, length us, event | category | flops | bytes accessed | tf_op | source)
XLA Modules:
  0.0 36.4 jit_solution(1394660035044383170)
XLA Ops:
  0.6 1.1 %prep.1 = (bf16[8,1152]{1,0:T(8,128)(2,1)S(1)}, bf16[8,1152]{1,0:T(8,128)(2,1)S(1)}, bf16[8,1152]{1,0:T(8,128)(2,1)S(1)}, bf16[8,1152]{1,0:T(8,128)(2,1)S(1)}) custom-call(s32[8]{0:T(128)} %refs_0_.1, f32[1,128]{1,0:T(1,128)} %constant.2.clone.refs_1_, bf16[8,1536]{1,0:T(8,128)(2,1)} %refs_2_.1, bf16[8,1536]{1,0:T(8,128)(2,1)} %refs_3_.1, ...), custom_call_target="tpu_custom_call" | custom-call | tf_op jit(solution)/shard_map/prep/pallas_call | solution.py:80
  1.7 2.7 %collective-permute-start = (bf16[8,1152]{1,0:T(8,128)(2,1)S(1)}, bf16[8,1152]{1,0:T(8,128)(2,1)S(1)}, u32[]{:S(2)}, u32[]{:S(2)}) collective-permute-start(bf16[8,1152]{1,0:T(8,128)(2,1)S(1)} %get-tuple-element.13), channel_id=1, source_target_pairs={{0,17},{1,16},{2,19},{3,18},{4,21},{5,20},{6,23},{7,22},{8,25},{9,... | collective-permute-start | bytes 55304 | tf_op jit(solution)/shard_map/ppermute | solution.py:71
  4.4 0.4 %collective-permute-start.1 = (bf16[8,1152]{1,0:T(8,128)(2,1)S(1)}, bf16[8,1152]{1,0:T(8,128)(2,1)S(1)}, u32[]{:S(2)}, u32[]{:S(2)}) collective-permute-start(bf16[8,1152]{1,0:T(8,128)(2,1)S(1)} %get-tuple-element.14), channel_id=1, source_target_pairs={{0,1},{1,0},{2,3},{3,2},{4,5},{5,4},{6,7},{7,6},{8,9},{9,8},{10,11... | collective-permute-start | bytes 55304 | tf_op jit(solution)/shard_map/ppermute | solution.py:71
  4.9 0.4 %collective-permute-start.2 = (bf16[8,1152]{1,0:T(8,128)(2,1)S(1)}, bf16[8,1152]{1,0:T(8,128)(2,1)S(1)}, u32[]{:S(2)}, u32[]{:S(2)}) collective-permute-start(bf16[8,1152]{1,0:T(8,128)(2,1)S(1)} %get-tuple-element.15), channel_id=1, source_target_pairs={{0,16},{1,17},{2,18},{3,19},{4,20},{5,21},{6,22},{7,23},{8,24},{9,... | collective-permute-start | bytes 55304 | tf_op jit(solution)/shard_map/ppermute | solution.py:71
  5.9 1.4 %text.1 = (bf16[128,384]{1,0:T(8,128)(2,1)S(1)}, bf16[128,384]{1,0:T(8,128)(2,1)S(1)}, bf16[128,384]{1,0:T(8,128)(2,1)S(1)}, f32[8,128]{1,0:T(8,128)S(1)}) custom-call(bf16[512,1536]{1,0:T(8,128)(2,1)} %q_h.1, bf16[512,1536]{1,0:T(8,128)(2,1)} %k_h.1, bf16[512,1536]{1,0:T(8,128)(2,1)} %v_h.1, f32[1,128]{1,0:T(1,128)} %bitcast.6, f32[1,128]{1,0:T(1,128)} %bitcast.7, ...), custom_call_target="tpu_custom_call" | custom-call | flops 20000000 | bytes 600000 | tf_op jit(solution)/shard_map/text/pallas_call | solution.py:80
  7.3 0.0 collective-permute-done.a1
  7.3 0.8 %collective-permute-done.1.a2 = bf16[8,1152]{1,0:T(8,128)(2,1)S(1)} collective-permute-done((bf16[8,1152]{1,0:T(8,128)(2,1)S(1)}, bf16[8,1152]{1,0:T(8,128)(2,1)S(1)}, u32[]{:S(2)}, u32[]{:S(2)}) %collective-permute-start.1) | collective-permute-done | bytes 18464 | tf_op jit(solution)/shard_map/ppermute | solution.py:71
  8.2 0.4 %collective-permute-done.2.a3 = bf16[8,1152]{1,0:T(8,128)(2,1)S(1)} collective-permute-done((bf16[8,1152]{1,0:T(8,128)(2,1)S(1)}, bf16[8,1152]{1,0:T(8,128)(2,1)S(1)}, u32[]{:S(2)}, u32[]{:S(2)}) %collective-permute-start.2) | collective-permute-done | bytes 18464 | tf_op jit(solution)/shard_map/ppermute | solution.py:71
  8.6 3.0 %collective-permute-start.6 = (bf16[32,384]{1,0:T(8,128)(2,1)S(1)}, bf16[32,384]{1,0:T(8,128)(2,1)S(1)}, u32[]{:S(2)}, u32[]{:S(2)}) collective-permute-start(bf16[32,384]{1,0:T(8,128)(2,1)S(1)} %get-tuple-element.18.a), channel_id=1, source_target_pairs={{0,3},{1,2},{2,1},{3,0},{4,7},{5,6},{6,5},{7,4},{8,11},{9,10},{10,... | collective-permute-start | bytes 73736 | tf_op jit(solution)/shard_map/ppermute | solution.py:71
  11.6 2.1 %collective-permute-start.5 = (bf16[32,768]{1,0:T(8,128)(2,1)S(1)}, bf16[32,768]{1,0:T(8,128)(2,1)S(1)}, u32[]{:S(2)}, u32[]{:S(2)}) collective-permute-start(bf16[32,768]{1,0:T(8,128)(2,1)S(1)} %get-tuple-element.17.kv0), channel_id=1, source_target_pairs={{0,48},{1,49},{2,50},{3,51},{4,52},{5,53},{6,54},{7,55},{8,56},{9,... | collective-permute-start | bytes 147464 | tf_op jit(solution)/shard_map/ppermute | solution.py:71
  13.7 4.0 %collective-permute-start.4 = (bf16[32,768]{1,0:T(8,128)(2,1)S(1)}, bf16[32,768]{1,0:T(8,128)(2,1)S(1)}, u32[]{:S(2)}, u32[]{:S(2)}) collective-permute-start(bf16[32,768]{1,0:T(8,128)(2,1)S(1)} %get-tuple-element.17.kv0), channel_id=1, source_target_pairs={{0,12},{1,13},{2,14},{3,15},{4,8},{5,9},{6,10},{7,11},{8,4},{9,5},... | collective-permute-start | bytes 147464 | tf_op jit(solution)/shard_map/ppermute | solution.py:71
  17.8 0.6 %collective-permute-start.3 = (bf16[32,768]{1,0:T(8,128)(2,1)S(1)}, bf16[32,768]{1,0:T(8,128)(2,1)S(1)}, u32[]{:S(2)}, u32[]{:S(2)}) collective-permute-start(bf16[32,768]{1,0:T(8,128)(2,1)S(1)} %get-tuple-element.17.kv0), channel_id=1, source_target_pairs={{0,60},{1,61},{2,62},{3,63},{4,56},{5,57},{6,58},{7,59},{8,52},{9,... | collective-permute-start | bytes 147464 | tf_op jit(solution)/shard_map/ppermute | solution.py:71
  18.4 0.0 collective-permute-done.6.b
  18.4 0.1 collective-permute-start.7
  18.5 0.0 collective-permute-done.5.kv3
  18.5 1.4 %collective-permute-done.4.kv2 = bf16[32,768]{1,0:T(8,128)(2,1)S(1)} collective-permute-done((bf16[32,768]{1,0:T(8,128)(2,1)S(1)}, bf16[32,768]{1,0:T(8,128)(2,1)S(1)}, u32[]{:S(2)}, u32[]{:S(2)}) %collective-permute-start.4) | collective-permute-done | bytes 49184 | tf_op jit(solution)/shard_map/ppermute | solution.py:71
  19.8 5.3 %collective-permute-done.3.kv1 = bf16[32,768]{1,0:T(8,128)(2,1)S(1)} collective-permute-done((bf16[32,768]{1,0:T(8,128)(2,1)S(1)}, bf16[32,768]{1,0:T(8,128)(2,1)S(1)}, u32[]{:S(2)}, u32[]{:S(2)}) %collective-permute-start.3) | collective-permute-done | bytes 49184 | tf_op jit(solution)/shard_map/ppermute | solution.py:71
  25.2 0.0 collective-permute-done.7.q1
  25.2 0.8 %attend.1 = bf16[16,16,512]{2,1,0:T(8,128)(2,1)S(1)} custom-call(bf16[32,768]{1,0:T(8,128)(2,1)S(1)} %get-tuple-element.17.kv0, bf16[32,768]{1,0:T(8,128)(2,1)S(1)} %collective-permute-done.3.kv1, bf16[32,768]{1,0:T(8,128)(2,1)S(1)} %collective-permute-done.4.kv2, bf16[32,768]{1,0:T(8,128)(2,1)S(1)} %collective-permute-done.5.kv3, ...), custom_call_target="tpu_custom_call" | custom-call | tf_op jit(solution)/shard_map/attend/pallas_call | solution.py:353
  26.0 9.4 %all_to_all.5.got = bf16[16,16,512]{2,1,0:T(8,128)(2,1)S(1)} all-to-all(bf16[16,16,512]{2,1,0:T(8,128)(2,1)S(1)} %attend.1), channel_id=1, replica_groups={{16,0,17,1,18,2,19,3,20,4,21,5,22,6,23,7},{28,12,29,13,30,14,31,15,24,8..., dimensions={0} | all-to-all | bytes 524288 | tf_op jit(solution)/shard_map/all_to_all | solution.py:361
  35.4 0.9 %combine.1 = (bf16[8,1536]{1,0:T(8,128)(2,1)}, bf16[8,1536]{1,0:T(8,128)(2,1)}) custom-call(bf16[16,16,512]{2,1,0:T(8,128)(2,1)S(1)} %all_to_all.5.got), custom_call_target="tpu_custom_call" | custom-call | tf_op jit(solution)/shard_map/combine/pallas_call | solution.py:363
  (2 shorter events, 0.0 us)
Async XLA Ops:
  1.7 5.6 %collective-permute-start = (bf16[8,1152]{1,0:T(8,128)(2,1)S(1)}, bf16[8,1152]{1,0:T(8,128)(2,1)S(1)}, u32[]{:S(2)}, u32[]{:S(2)}) collective-permute-start(bf16[8,1152]{1,0:T(8,128)(2,1)S(1)} %get-tuple-element.13), channel_id=1, source_target_pairs={{0,17},{1,16},{2,19},{3,18},{4,21},{5,20},{6,23},{7,22},{8,25},{9,... | collective-permute-start | bytes 55304 | tf_op jit(solution)/shard_map/ppermute | solution.py:71
  4.4 3.8 %collective-permute-start.1 = (bf16[8,1152]{1,0:T(8,128)(2,1)S(1)}, bf16[8,1152]{1,0:T(8,128)(2,1)S(1)}, u32[]{:S(2)}, u32[]{:S(2)}) collective-permute-start(bf16[8,1152]{1,0:T(8,128)(2,1)S(1)} %get-tuple-element.14), channel_id=1, source_target_pairs={{0,1},{1,0},{2,3},{3,2},{4,5},{5,4},{6,7},{7,6},{8,9},{9,8},{10,11... | collective-permute-start | bytes 55304 | tf_op jit(solution)/shard_map/ppermute | solution.py:71
  4.9 3.8 %collective-permute-start.2 = (bf16[8,1152]{1,0:T(8,128)(2,1)S(1)}, bf16[8,1152]{1,0:T(8,128)(2,1)S(1)}, u32[]{:S(2)}, u32[]{:S(2)}) collective-permute-start(bf16[8,1152]{1,0:T(8,128)(2,1)S(1)} %get-tuple-element.15), channel_id=1, source_target_pairs={{0,16},{1,17},{2,18},{3,19},{4,20},{5,21},{6,22},{7,23},{8,24},{9,... | collective-permute-start | bytes 55304 | tf_op jit(solution)/shard_map/ppermute | solution.py:71
  8.6 9.7 %collective-permute-start.6 = (bf16[32,384]{1,0:T(8,128)(2,1)S(1)}, bf16[32,384]{1,0:T(8,128)(2,1)S(1)}, u32[]{:S(2)}, u32[]{:S(2)}) collective-permute-start(bf16[32,384]{1,0:T(8,128)(2,1)S(1)} %get-tuple-element.18.a), channel_id=1, source_target_pairs={{0,3},{1,2},{2,1},{3,0},{4,7},{5,6},{6,5},{7,4},{8,11},{9,10},{10,... | collective-permute-start | bytes 73736 | tf_op jit(solution)/shard_map/ppermute | solution.py:71
  11.6 6.8 %collective-permute-start.5 = (bf16[32,768]{1,0:T(8,128)(2,1)S(1)}, bf16[32,768]{1,0:T(8,128)(2,1)S(1)}, u32[]{:S(2)}, u32[]{:S(2)}) collective-permute-start(bf16[32,768]{1,0:T(8,128)(2,1)S(1)} %get-tuple-element.17.kv0), channel_id=1, source_target_pairs={{0,48},{1,49},{2,50},{3,51},{4,52},{5,53},{6,54},{7,55},{8,56},{9,... | collective-permute-start | bytes 147464 | tf_op jit(solution)/shard_map/ppermute | solution.py:71
  13.7 6.1 %collective-permute-start.4 = (bf16[32,768]{1,0:T(8,128)(2,1)S(1)}, bf16[32,768]{1,0:T(8,128)(2,1)S(1)}, u32[]{:S(2)}, u32[]{:S(2)}) collective-permute-start(bf16[32,768]{1,0:T(8,128)(2,1)S(1)} %get-tuple-element.17.kv0), channel_id=1, source_target_pairs={{0,12},{1,13},{2,14},{3,15},{4,8},{5,9},{6,10},{7,11},{8,4},{9,5},... | collective-permute-start | bytes 147464 | tf_op jit(solution)/shard_map/ppermute | solution.py:71
  17.8 7.4 %collective-permute-start.3 = (bf16[32,768]{1,0:T(8,128)(2,1)S(1)}, bf16[32,768]{1,0:T(8,128)(2,1)S(1)}, u32[]{:S(2)}, u32[]{:S(2)}) collective-permute-start(bf16[32,768]{1,0:T(8,128)(2,1)S(1)} %get-tuple-element.17.kv0), channel_id=1, source_target_pairs={{0,60},{1,61},{2,62},{3,63},{4,56},{5,57},{6,58},{7,59},{8,52},{9,... | collective-permute-start | bytes 147464 | tf_op jit(solution)/shard_map/ppermute | solution.py:71
  18.4 6.8 %collective-permute-start.7 = (bf16[64,384]{1,0:T(8,128)(2,1)S(1)}, bf16[64,384]{1,0:T(8,128)(2,1)S(1)}, u32[]{:S(2)}, u32[]{:S(2)}) collective-permute-start(bf16[64,384]{1,0:T(8,128)(2,1)S(1)} %join.1.q0), channel_id=1, source_target_pairs={{0,4},{1,5},{2,6},{3,7},{4,0},{5,1},{6,2},{7,3},{8,12},{9,13},{10,... | collective-permute-start | bytes 147464 | tf_op jit(solution)/shard_map/ppermute | solution.py:71

commit v2 on v1

--- a/solution.py
+++ b/solution.py
@@ -191,22 +191,18 @@
     bias[...] = jnp.where(key < length[0], 0.0, MASKED)
 
 
-def attend_kernel(kv0, kv1, kv2, kv3, q0, q1, qt, kt, vt, bias, out):
-    kvs, qs = (kv0, kv1, kv2, kv3), (q0, q1)
-    width = qt.shape[1]
-    heads = width // HD
+def attend(queries, kvs, kt, vt, bias, base):
+    width = kt.shape[1]
     text_keys = kt.shape[0]
-    image_rows = 2 * q0.shape[0]
-    rows = image_rows + qt.shape[0]
-    x, z, y = split_index(lax.axis_index("seq"))
     masked = bias[0:1, :]
-    lane = lax.broadcasted_iota(jnp.int32, (rows, HD), 1)
+    rows = sum(r.shape[0] for r in queries)
+    lane = lax.broadcasted_iota(jnp.int32, (rows, HD), 1) - base
     stats = jnp.zeros((rows, HD), jnp.float32)
     blended = []
-    for h in range(heads):
+    for h in range(width // HD):
         cols = slice(h * HD, (h + 1) * HD)
         vcols = slice(width + h * HD, width + (h + 1) * HD)
-        query = jnp.concatenate([r[:, cols] for r in qs] + [qt[:, cols]], axis=0)
+        query = jnp.concatenate([r[:, cols] for r in queries], axis=0)
         key = jnp.concatenate([kt[:, cols]] + [r[:, cols] for r in kvs], axis=0)
         value = jnp.concatenate([vt[:, cols]] + [r[:, vcols] for r in kvs], axis=0)
         s = lax.dot_general(query, key, (((1,), (1,)), ((), ())), preferred_element_type=jnp.float32)
@@ -216,52 +212,75 @@
         m = m * SCALE
         l = jnp.sum(e, axis=1, keepdims=True)
         blended.append(jnp.dot(e.astype(jnp.bfloat16), value, preferred_element_type=jnp.float32))
-        for first, value in ((h, m), (24 + h, l)):
-            for piece in range(3 if first == h else 2):
+        for first, value, pieces in ((h, m, 3), (24 + h, l, 2)):
+            for piece in range(pieces):
                 stats = jnp.where(lane == first + 8 * piece, value, stats)
                 value = value - value.astype(jnp.bfloat16).astype(jnp.float32)
-    blended.append(stats)
+    return blended + [stats]
+
+
+def attend_kernel(kv0, kv1, kv2, kv3, q0, q1, qt, kt, vt, bias, out):
+    kvs = (kv0, kv1, kv2, kv3)
+    half = HD // 2
+    heads = qt.shape[1] // HD
+    x, z, y = split_index(lax.axis_index("seq"))
+    text = attend((qt,), kvs, kt, vt, bias, half)
+    for j in range(out.shape[0]):
+        for c, part in enumerate(text):
+            rows = part[j * 8 : (j + 1) * 8].astype(jnp.bfloat16)
+            if c < heads:
+                out[j, :, (heads + c) * HD : (heads + c + 1) * HD] = rows
+            else:
+                out[j, :, 2 * heads * HD + half :] = rows[:, half:]
+    image = attend((q0, q1), kvs, kt, vt, bias, 0)
     for a, key_step in enumerate(QUERY_STEPS):
         for b, head_step in enumerate(HEAD_STEPS):
             i = a * SIDE + b
             there = member(x ^ key_step[0], z ^ key_step[1] ^ head_step[1], y ^ head_step[2])
-            for c, part in enumerate(blended):
-                cols = slice(c * HD, (c + 1) * HD)
-                out[there, 0:8, cols] = part[i * 8 : (i + 1) * 8].astype(jnp.bfloat16)
-                begin = image_rows + i * 8
-                out[i, 8:16, cols] = part[begin : begin + 8].astype(jnp.bfloat16)
-
-
-def combine_kernel(got, image_out, text_out):
-    heads = (got.shape[2] - HD) // HD
+            for c, part in enumerate(image):
+                rows = part[i * 8 : (i + 1) * 8].astype(jnp.bfloat16)
+                if c < heads:
+                    out[there, :, c * HD : (c + 1) * HD] = rows
+                else:
+                    out[there, :, 2 * heads * HD : 2 * heads * HD + half] = rows[:, :half]
+
+
+def combine_kernel(got, image_out, text_out, image_s, text_s, sems):
+    heads = (got.shape[2] - HD) // HD // 2
     width = heads * HD
-    half = image_out.shape[0]
+    rows = got.shape[1]
     members = [[None] * SIDE for _ in range(SIDE)]
     for j in range(got.shape[0]):
         px, z, py = j >> 3, (j >> 1) & 3, (j & 1) ^ 1
         members[px * 2 + (z >> 1)][parity(z) * 2 + py] = j
 
-    def stacked(key, cols):
+    def stacked(key, block):
+        cols = slice(block * HD, (block + 1) * HD)
         return jnp.concatenate([got[m, :, cols].astype(jnp.float32) for m in members[key]], axis=0)
 
-    stats = [stacked(key, slice(width, width + HD)) for key in range(SIDE)]
+    stats = [stacked(key, 2 * heads) for key in range(SIDE)]
     peaks = [s + pltpu.roll(s, HD - 8, 1) + pltpu.roll(s, HD - 16, 1) for s in stats]
     sums = [pltpu.roll(s, HD - 24, 1) + pltpu.roll(s, HD - 32, 1) for s in stats]
     top = jnp.maximum(jnp.maximum(peaks[0], peaks[1]), jnp.maximum(peaks[2], peaks[3]))
     factors = [jnp.exp(p - top) for p in peaks]
     total = factors[0] * sums[0] + factors[1] * sums[1] + factors[2] * sums[2] + factors[3] * sums[3]
-    lane = lax.broadcasted_iota(jnp.int32, total.shape, 1)
+    lane = lax.broadcasted_iota(jnp.int32, total.shape, 1) & (HD // 2 - 1)
     inverse = 1.0 / jnp.where(lane < heads, total, 1.0)
     weights = [f * inverse for f in factors]
-    for h in range(heads):
-        acc = 0.0
-        for key in range(SIDE):
-            acc = acc + stacked(key, slice(h * HD, (h + 1) * HD)) * weights[key][:, h : h + 1]
-        for g in range(SIDE):
-            cols = slice(g * width + h * HD, g * width + (h + 1) * HD)
-            rows = acc[g * 2 * half : (g + 1) * 2 * half].astype(jnp.bfloat16)
-            image_out[:, cols] = rows[:half]
-            text_out[:, cols] = rows[half:]
+    copies = []
+    for t, (dst, scratch) in enumerate(((image_out, image_s), (text_out, text_s))):
+        for h in range(heads):
+            at = t * (HD // 2) + h
+            acc = 0.0
+            for key in range(SIDE):
+                acc = acc + stacked(key, t * heads + h) * weights[key][:, at : at + 1]
+            for g in range(SIDE):
+                cols = slice(g * width + h * HD, g * width + (h + 1) * HD)
+                scratch[:, cols] = acc[g * rows : (g + 1) * rows].astype(jnp.bfloat16)
+        copies.append(pltpu.make_async_copy(scratch, dst, sems.at[t]))
+        copies[-1].start()
+    for c in copies:
+        c.wait()
 
 
 def local(
@@ -349,10 +368,9 @@
     )(q, q_next)
     q_last = exchange(q_two, QUERY_STEPS[2])
 
-    out_rows = rows + text_rows // SIDE**3
     partial = pl.pallas_call(
         attend_kernel,
-        out_shape=pltpu.VMEM((parts, out_rows, width + HD), bf),
+        out_shape=pltpu.VMEM((parts, rows, 2 * width + HD), bf),
         in_specs=[VM] * 10,
         out_specs=VM,
         name="attend",
@@ -360,11 +378,17 @@
 
     got = in_vmem(lax.all_to_all(partial, "seq", 0, 0, axis_index_groups=query_groups(), tiled=True))
 
+    own_text = text_rows // SIDE**3
     return pl.pallas_call(
         combine_kernel,
-        out_shape=[struct((rows, model), bf), struct((out_rows - rows, model), bf)],
+        out_shape=[struct((rows, model), bf), struct((own_text, model), bf)],
         in_specs=[VM],
-        out_specs=[VM] * 2,
+        out_specs=[HB] * 2,
+        scratch_shapes=[
+            pltpu.VMEM((rows, model), bf),
+            pltpu.VMEM((own_text, model), bf),
+            pltpu.SemaphoreType.DMA((2,)),
+        ],
         name="combine",
     )(got)
 

time: 36.6 us -> 36.5 us (level)
  no operation moved by 1% of the time
where the time goes in v2:
time: 36.5 us; the launch traced here: 36.3 us
  starting transfers between devices  13.4 us (37%)
  blocking collectives  9.39 us (26%)
  waiting for transfers between devices  8.01 us (22%)
  Pallas kernels  4.18 us (11%)
  between operations  1.34 us (4%)
    ppermute x8, starting transfers between devices, exchange(): return in_vmem(lax.ppermute(value, 'seq', pairs))  13.4 us
    all_to_all x1, blocking collectives, local(): lax.all_to_all(partial, 'seq', 0, 0, axis_index_groups=query_groups(), ti...  9.39 us
    ppermute x8, waiting for transfers between devices, exchange(): return in_vmem(lax.ppermute(value, 'seq', pairs))  8.01 us
    pallas_call x4, Pallas kernels, vmem_call(): return lambda *args: jax.tree.map(in_vmem, call(*args))  2.47 us
    pallas_call x1, Pallas kernels, local(): pl.pallas_call(combine_kernel, out_shape=[struct((rows, model), bf), stru...  0.92 us
    pallas_call x1, Pallas kernels, local(): pl.pallas_call(attend_kernel, out_shape=pltpu.VMEM((parts, rows, 2 * widt...  0.79 us
  transfers between devices with their start and end apart: 8, of which 4 were waited for; matrix products, arithmetic and copies ran while one was open for 0% of the time, Pallas kernels for 4%

profile of v2, /device:TPU:0, one launch (start us, length us, event | category | flops | bytes accessed | tf_op | source)
XLA Modules:
  0.0 36.3 jit_solution(11791269199012881338)
XLA Ops:
  0.6 1.1 %prep.1 = (bf16[8,1152]{1,0:T(8,128)(2,1)S(1)}, bf16[8,1152]{1,0:T(8,128)(2,1)S(1)}, bf16[8,1152]{1,0:T(8,128)(2,1)S(1)}, bf16[8,1152]{1,0:T(8,128)(2,1)S(1)}) custom-call(s32[8]{0:T(128)} %refs_0_.1, f32[1,128]{1,0:T(1,128)} %constant.2.clone.refs_1_, bf16[8,1536]{1,0:T(8,128)(2,1)} %refs_2_.1, bf16[8,1536]{1,0:T(8,128)(2,1)} %refs_3_.1, ...), custom_call_target="tpu_custom_call" | custom-call | tf_op jit(solution)/shard_map/prep/pallas_call | solution.py:80
  1.7 2.7 %collective-permute-start = (bf16[8,1152]{1,0:T(8,128)(2,1)S(1)}, bf16[8,1152]{1,0:T(8,128)(2,1)S(1)}, u32[]{:S(2)}, u32[]{:S(2)}) collective-permute-start(bf16[8,1152]{1,0:T(8,128)(2,1)S(1)} %get-tuple-element.13), channel_id=1, source_target_pairs={{0,17},{1,16},{2,19},{3,18},{4,21},{5,20},{6,23},{7,22},{8,25},{9,... | collective-permute-start | bytes 55304 | tf_op jit(solution)/shard_map/ppermute | solution.py:71
  4.4 0.4 %collective-permute-start.1 = (bf16[8,1152]{1,0:T(8,128)(2,1)S(1)}, bf16[8,1152]{1,0:T(8,128)(2,1)S(1)}, u32[]{:S(2)}, u32[]{:S(2)}) collective-permute-start(bf16[8,1152]{1,0:T(8,128)(2,1)S(1)} %get-tuple-element.14), channel_id=1, source_target_pairs={{0,1},{1,0},{2,3},{3,2},{4,5},{5,4},{6,7},{7,6},{8,9},{9,8},{10,11... | collective-permute-start | bytes 55304 | tf_op jit(solution)/shard_map/ppermute | solution.py:71
  4.9 0.4 %collective-permute-start.2 = (bf16[8,1152]{1,0:T(8,128)(2,1)S(1)}, bf16[8,1152]{1,0:T(8,128)(2,1)S(1)}, u32[]{:S(2)}, u32[]{:S(2)}) collective-permute-start(bf16[8,1152]{1,0:T(8,128)(2,1)S(1)} %get-tuple-element.15), channel_id=1, source_target_pairs={{0,16},{1,17},{2,18},{3,19},{4,20},{5,21},{6,22},{7,23},{8,24},{9,... | collective-permute-start | bytes 55304 | tf_op jit(solution)/shard_map/ppermute | solution.py:71
  5.9 1.4 %text.1 = (bf16[128,384]{1,0:T(8,128)(2,1)S(1)}, bf16[128,384]{1,0:T(8,128)(2,1)S(1)}, bf16[128,384]{1,0:T(8,128)(2,1)S(1)}, f32[8,128]{1,0:T(8,128)S(1)}) custom-call(bf16[512,1536]{1,0:T(8,128)(2,1)} %q_h.1, bf16[512,1536]{1,0:T(8,128)(2,1)} %k_h.1, bf16[512,1536]{1,0:T(8,128)(2,1)} %v_h.1, f32[1,128]{1,0:T(1,128)} %bitcast.6, f32[1,128]{1,0:T(1,128)} %bitcast.7, ...), custom_call_target="tpu_custom_call" | custom-call | flops 20000000 | bytes 600000 | tf_op jit(solution)/shard_map/text/pallas_call | solution.py:80
  7.3 0.0 collective-permute-done.a1
  7.3 0.8 %collective-permute-done.1.a2 = bf16[8,1152]{1,0:T(8,128)(2,1)S(1)} collective-permute-done((bf16[8,1152]{1,0:T(8,128)(2,1)S(1)}, bf16[8,1152]{1,0:T(8,128)(2,1)S(1)}, u32[]{:S(2)}, u32[]{:S(2)}) %collective-permute-start.1) | collective-permute-done | bytes 18464 | tf_op jit(solution)/shard_map/ppermute | solution.py:71
  8.2 0.4 %collective-permute-done.2.a3 = bf16[8,1152]{1,0:T(8,128)(2,1)S(1)} collective-permute-done((bf16[8,1152]{1,0:T(8,128)(2,1)S(1)}, bf16[8,1152]{1,0:T(8,128)(2,1)S(1)}, u32[]{:S(2)}, u32[]{:S(2)}) %collective-permute-start.2) | collective-permute-done | bytes 18464 | tf_op jit(solution)/shard_map/ppermute | solution.py:71
  8.6 3.0 %collective-permute-start.6 = (bf16[32,384]{1,0:T(8,128)(2,1)S(1)}, bf16[32,384]{1,0:T(8,128)(2,1)S(1)}, u32[]{:S(2)}, u32[]{:S(2)}) collective-permute-start(bf16[32,384]{1,0:T(8,128)(2,1)S(1)} %get-tuple-element.18.a), channel_id=1, source_target_pairs={{0,3},{1,2},{2,1},{3,0},{4,7},{5,6},{6,5},{7,4},{8,11},{9,10},{10,... | collective-permute-start | bytes 73736 | tf_op jit(solution)/shard_map/ppermute | solution.py:71
  11.6 2.1 %collective-permute-start.5 = (bf16[32,768]{1,0:T(8,128)(2,1)S(1)}, bf16[32,768]{1,0:T(8,128)(2,1)S(1)}, u32[]{:S(2)}, u32[]{:S(2)}) collective-permute-start(bf16[32,768]{1,0:T(8,128)(2,1)S(1)} %get-tuple-element.17.kv0), channel_id=1, source_target_pairs={{0,48},{1,49},{2,50},{3,51},{4,52},{5,53},{6,54},{7,55},{8,56},{9,... | collective-permute-start | bytes 147464 | tf_op jit(solution)/shard_map/ppermute | solution.py:71
  13.7 4.0 %collective-permute-start.4 = (bf16[32,768]{1,0:T(8,128)(2,1)S(1)}, bf16[32,768]{1,0:T(8,128)(2,1)S(1)}, u32[]{:S(2)}, u32[]{:S(2)}) collective-permute-start(bf16[32,768]{1,0:T(8,128)(2,1)S(1)} %get-tuple-element.17.kv0), channel_id=1, source_target_pairs={{0,12},{1,13},{2,14},{3,15},{4,8},{5,9},{6,10},{7,11},{8,4},{9,5},... | collective-permute-start | bytes 147464 | tf_op jit(solution)/shard_map/ppermute | solution.py:71
  17.8 0.6 %collective-permute-start.3 = (bf16[32,768]{1,0:T(8,128)(2,1)S(1)}, bf16[32,768]{1,0:T(8,128)(2,1)S(1)}, u32[]{:S(2)}, u32[]{:S(2)}) collective-permute-start(bf16[32,768]{1,0:T(8,128)(2,1)S(1)} %get-tuple-element.17.kv0), channel_id=1, source_target_pairs={{0,60},{1,61},{2,62},{3,63},{4,56},{5,57},{6,58},{7,59},{8,52},{9,... | collective-permute-start | bytes 147464 | tf_op jit(solution)/shard_map/ppermute | solution.py:71
  18.4 0.0 collective-permute-done.6.b
  18.4 0.1 collective-permute-start.7
  18.5 0.0 collective-permute-done.5.kv3
  18.5 1.4 %collective-permute-done.4.kv2 = bf16[32,768]{1,0:T(8,128)(2,1)S(1)} collective-permute-done((bf16[32,768]{1,0:T(8,128)(2,1)S(1)}, bf16[32,768]{1,0:T(8,128)(2,1)S(1)}, u32[]{:S(2)}, u32[]{:S(2)}) %collective-permute-start.4) | collective-permute-done | bytes 49184 | tf_op jit(solution)/shard_map/ppermute | solution.py:71
  19.8 5.3 %collective-permute-done.3.kv1 = bf16[32,768]{1,0:T(8,128)(2,1)S(1)} collective-permute-done((bf16[32,768]{1,0:T(8,128)(2,1)S(1)}, bf16[32,768]{1,0:T(8,128)(2,1)S(1)}, u32[]{:S(2)}, u32[]{:S(2)}) %collective-permute-start.3) | collective-permute-done | bytes 49184 | tf_op jit(solution)/shard_map/ppermute | solution.py:71
  25.2 0.0 collective-permute-done.7.q1
  25.2 0.8 %attend.1 = bf16[16,8,896]{2,1,0:T(8,128)(2,1)S(1)} custom-call(bf16[32,768]{1,0:T(8,128)(2,1)S(1)} %get-tuple-element.17.kv0, bf16[32,768]{1,0:T(8,128)(2,1)S(1)} %collective-permute-done.3.kv1, bf16[32,768]{1,0:T(8,128)(2,1)S(1)} %collective-permute-done.4.kv2, bf16[32,768]{1,0:T(8,128)(2,1)S(1)} %collective-permute-done.5.kv3, ...), custom_call_target="tpu_custom_call" | custom-call | tf_op jit(solution)/shard_map/attend/pallas_call | solution.py:371
  26.0 9.4 %all_to_all.5.got = bf16[16,8,896]{2,1,0:T(8,128)(2,1)S(1)} all-to-all(bf16[16,8,896]{2,1,0:T(8,128)(2,1)S(1)} %attend.1), channel_id=1, replica_groups={{16,0,17,1,18,2,19,3,20,4,21,5,22,6,23,7},{28,12,29,13,30,14,31,15,24,8..., dimensions={0} | all-to-all | bytes 458752 | tf_op jit(solution)/shard_map/all_to_all | solution.py:379
  35.4 0.9 %combine.1 = (bf16[8,1536]{1,0:T(8,128)(2,1)}, bf16[8,1536]{1,0:T(8,128)(2,1)}) custom-call(bf16[16,8,896]{2,1,0:T(8,128)(2,1)S(1)} %all_to_all.5.got), custom_call_target="tpu_custom_call" | custom-call | tf_op jit(solution)/shard_map/combine/pallas_call | solution.py:382
  (2 shorter events, 0.0 us)
Async XLA Ops:
  1.7 5.6 %collective-permute-start = (bf16[8,1152]{1,0:T(8,128)(2,1)S(1)}, bf16[8,1152]{1,0:T(8,128)(2,1)S(1)}, u32[]{:S(2)}, u32[]{:S(2)}) collective-permute-start(bf16[8,1152]{1,0:T(8,128)(2,1)S(1)} %get-tuple-element.13), channel_id=1, source_target_pairs={{0,17},{1,16},{2,19},{3,18},{4,21},{5,20},{6,23},{7,22},{8,25},{9,... | collective-permute-start | bytes 55304 | tf_op jit(solution)/shard_map/ppermute | solution.py:71
  4.4 3.8 %collective-permute-start.1 = (bf16[8,1152]{1,0:T(8,128)(2,1)S(1)}, bf16[8,1152]{1,0:T(8,128)(2,1)S(1)}, u32[]{:S(2)}, u32[]{:S(2)}) collective-permute-start(bf16[8,1152]{1,0:T(8,128)(2,1)S(1)} %get-tuple-element.14), channel_id=1, source_target_pairs={{0,1},{1,0},{2,3},{3,2},{4,5},{5,4},{6,7},{7,6},{8,9},{9,8},{10,11... | collective-permute-start | bytes 55304 | tf_op jit(solution)/shard_map/ppermute | solution.py:71
  4.9 3.8 %collective-permute-start.2 = (bf16[8,1152]{1,0:T(8,128)(2,1)S(1)}, bf16[8,1152]{1,0:T(8,128)(2,1)S(1)}, u32[]{:S(2)}, u32[]{:S(2)}) collective-permute-start(bf16[8,1152]{1,0:T(8,128)(2,1)S(1)} %get-tuple-element.15), channel_id=1, source_target_pairs={{0,16},{1,17},{2,18},{3,19},{4,20},{5,21},{6,22},{7,23},{8,24},{9,... | collective-permute-start | bytes 55304 | tf_op jit(solution)/shard_map/ppermute | solution.py:71
  8.6 9.7 %collective-permute-start.6 = (bf16[32,384]{1,0:T(8,128)(2,1)S(1)}, bf16[32,384]{1,0:T(8,128)(2,1)S(1)}, u32[]{:S(2)}, u32[]{:S(2)}) collective-permute-start(bf16[32,384]{1,0:T(8,128)(2,1)S(1)} %get-tuple-element.18.a), channel_id=1, source_target_pairs={{0,3},{1,2},{2,1},{3,0},{4,7},{5,6},{6,5},{7,4},{8,11},{9,10},{10,... | collective-permute-start | bytes 73736 | tf_op jit(solution)/shard_map/ppermute | solution.py:71
  11.6 6.8 %collective-permute-start.5 = (bf16[32,768]{1,0:T(8,128)(2,1)S(1)}, bf16[32,768]{1,0:T(8,128)(2,1)S(1)}, u32[]{:S(2)}, u32[]{:S(2)}) collective-permute-start(bf16[32,768]{1,0:T(8,128)(2,1)S(1)} %get-tuple-element.17.kv0), channel_id=1, source_target_pairs={{0,48},{1,49},{2,50},{3,51},{4,52},{5,53},{6,54},{7,55},{8,56},{9,... | collective-permute-start | bytes 147464 | tf_op jit(solution)/shard_map/ppermute | solution.py:71
  13.7 6.1 %collective-permute-start.4 = (bf16[32,768]{1,0:T(8,128)(2,1)S(1)}, bf16[32,768]{1,0:T(8,128)(2,1)S(1)}, u32[]{:S(2)}, u32[]{:S(2)}) collective-permute-start(bf16[32,768]{1,0:T(8,128)(2,1)S(1)} %get-tuple-element.17.kv0), channel_id=1, source_target_pairs={{0,12},{1,13},{2,14},{3,15},{4,8},{5,9},{6,10},{7,11},{8,4},{9,5},... | collective-permute-start | bytes 147464 | tf_op jit(solution)/shard_map/ppermute | solution.py:71
  17.8 7.4 %collective-permute-start.3 = (bf16[32,768]{1,0:T(8,128)(2,1)S(1)}, bf16[32,768]{1,0:T(8,128)(2,1)S(1)}, u32[]{:S(2)}, u32[]{:S(2)}) collective-permute-start(bf16[32,768]{1,0:T(8,128)(2,1)S(1)} %get-tuple-element.17.kv0), channel_id=1, source_target_pairs={{0,60},{1,61},{2,62},{3,63},{4,56},{5,57},{6,58},{7,59},{8,52},{9,... | collective-permute-start | bytes 147464 | tf_op jit(solution)/shard_map/ppermute | solution.py:71
  18.4 6.8 %collective-permute-start.7 = (bf16[64,384]{1,0:T(8,128)(2,1)S(1)}, bf16[64,384]{1,0:T(8,128)(2,1)S(1)}, u32[]{:S(2)}, u32[]{:S(2)}) collective-permute-start(bf16[64,384]{1,0:T(8,128)(2,1)S(1)} %join.1.q0), channel_id=1, source_target_pairs={{0,4},{1,5},{2,6},{3,7},{4,0},{5,1},{6,2},{7,3},{8,12},{9,13},{10,... | collective-permute-start | bytes 147464 | tf_op jit(solution)/shard_map/ppermute | solution.py:71

commit v3 on v2

--- a/solution.py
+++ b/solution.py
@@ -50,7 +50,7 @@
     return parity(x) * 8 + z * 2 + (parity(y) ^ 1)
 
 
-HEAD_STEPS = ((0, 0, 0), (0, 1, 1), (0, 1, 0), (0, 0, 1))
+HEAD_STEPS = ((0, 0, 0), (0, 1, 0), (0, 1, 1), (0, 0, 1))
 QUERY_STEPS = ((0, 0, 0), (0, 3, 0), (1, 0, 0), (1, 3, 0))
 KEY_STEPS = ((0, 0, 0), (3, 0, 3), (3, 0, 0), (0, 0, 3))
 
@@ -143,7 +143,7 @@
         out[:, 2 * width : 3 * width] = q_s[:, pl.ds(start, width)]
 
 
-def pack_kernel(a0, a1, a2, a3, order_only, kv, q):
+def pack_kernel(a0, a1, a2, a3, kv, q):
     rows = a0.shape[0]
     width = q.shape[1]
     for j, a in enumerate((a0, a1, a2, a3)):
@@ -198,21 +198,25 @@
     rows = sum(r.shape[0] for r in queries)
     lane = lax.broadcasted_iota(jnp.int32, (rows, HD), 1) - base
     stats = jnp.zeros((rows, HD), jnp.float32)
+    heads = range(width // HD)
+    scores = []
+    for h in heads:
+        cols = slice(h * HD, (h + 1) * HD)
+        query = jnp.concatenate([r[:, cols] for r in queries], axis=0)
+        key = jnp.concatenate([kt[:, cols]] + [r[:, cols] for r in kvs], axis=0)
+        s = lax.dot_general(query, key, (((1,), (1,)), ((), ())), preferred_element_type=jnp.float32)
+        scores.append(jnp.concatenate([s[:, :text_keys] + masked, s[:, text_keys:]], axis=1))
+    tops = [jnp.max(s, axis=1, keepdims=True) for s in scores]
+    weights = [jnp.exp2((s - m) * (SCALE * LOG2E)) for s, m in zip(scores, tops)]
     blended = []
-    for h in range(width // HD):
+    for h in heads:
         cols = slice(h * HD, (h + 1) * HD)
         vcols = slice(width + h * HD, width + (h + 1) * HD)
-        query = jnp.concatenate([r[:, cols] for r in queries], axis=0)
-        key = jnp.concatenate([kt[:, cols]] + [r[:, cols] for r in kvs], axis=0)
         value = jnp.concatenate([vt[:, cols]] + [r[:, vcols] for r in kvs], axis=0)
-        s = lax.dot_general(query, key, (((1,), (1,)), ((), ())), preferred_element_type=jnp.float32)
-        s = jnp.concatenate([s[:, :text_keys] + masked, s[:, text_keys:]], axis=1)
-        m = jnp.max(s, axis=1, keepdims=True)
-        e = jnp.exp2((s - m) * (SCALE * LOG2E))
-        m = m * SCALE
-        l = jnp.sum(e, axis=1, keepdims=True)
-        blended.append(jnp.dot(e.astype(jnp.bfloat16), value, preferred_element_type=jnp.float32))
-        for first, value, pieces in ((h, m, 3), (24 + h, l, 2)):
+        blended.append(jnp.dot(weights[h].astype(jnp.bfloat16), value, preferred_element_type=jnp.float32))
+    totals = [jnp.sum(e, axis=1, keepdims=True) for e in weights]
+    for h in heads:
+        for first, value, pieces in ((h, tops[h] * SCALE, 3), (24 + h, totals[h], 2)):
             for piece in range(pieces):
                 stats = jnp.where(lane == first + 8 * piece, value, stats)
                 value = value - value.astype(jnp.bfloat16).astype(jnp.float32)
@@ -350,10 +354,10 @@
     kv, q = vmem_call(
         pack_kernel,
         out_shape=[pltpu.VMEM((SIDE * rows, 2 * width), bf), pltpu.VMEM((SIDE * rows, width), bf)],
-        in_specs=[VM] * SIDE + [VM],
+        in_specs=[VM] * SIDE,
         out_specs=[VM] * 2,
         name="pack",
-    )(*from_y, bias)
+    )(*from_y)
 
     q_next = exchange(q, QUERY_STEPS[1])
     kvs = [kv]

time: 36.5 us -> 36.5 us (level)
  no operation moved by 1% of the time
where the time goes in v3:
time: 36.5 us; the launch traced here: 36.3 us
  starting transfers between devices  13.4 us (37%)
  blocking collectives  9.38 us (26%)
  waiting for transfers between devices  8.02 us (22%)
  Pallas kernels  4.14 us (11%)
  between operations  1.34 us (4%)
    ppermute x8, starting transfers between devices, exchange(): return in_vmem(lax.ppermute(value, 'seq', pairs))  13.4 us
    all_to_all x1, blocking collectives, local(): lax.all_to_all(partial, 'seq', 0, 0, axis_index_groups=query_groups(), ti...  9.38 us
    ppermute x8, waiting for transfers between devices, exchange(): return in_vmem(lax.ppermute(value, 'seq', pairs))  8.02 us
    pallas_call x4, Pallas kernels, vmem_call(): return lambda *args: jax.tree.map(in_vmem, call(*args))  2.46 us
    pallas_call x1, Pallas kernels, local(): pl.pallas_call(combine_kernel, out_shape=[struct((rows, model), bf), stru...  0.92 us
    pallas_call x1, Pallas kernels, local(): pl.pallas_call(attend_kernel, out_shape=pltpu.VMEM((parts, rows, 2 * widt...  0.75 us
  transfers between devices with their start and end apart: 8, of which 4 were waited for; matrix products, arithmetic and copies ran while one was open for 0% of the time, Pallas kernels for 4%

profile of v3, /device:TPU:0, one launch (start us, length us, event | category | flops | bytes accessed | tf_op | source)
XLA Modules:
  0.0 36.3 jit_solution(18430848260863668984)
XLA Ops:
  0.6 1.1 %prep.1 = (bf16[8,1152]{1,0:T(8,128)(2,1)S(1)}, bf16[8,1152]{1,0:T(8,128)(2,1)S(1)}, bf16[8,1152]{1,0:T(8,128)(2,1)S(1)}, bf16[8,1152]{1,0:T(8,128)(2,1)S(1)}) custom-call(s32[8]{0:T(128)} %refs_0_.1, f32[1,128]{1,0:T(1,128)} %constant.2.clone.refs_1_, bf16[8,1536]{1,0:T(8,128)(2,1)} %refs_2_.1, bf16[8,1536]{1,0:T(8,128)(2,1)} %refs_3_.1, ...), custom_call_target="tpu_custom_call" | custom-call | tf_op jit(solution)/shard_map/prep/pallas_call | solution.py:80
  1.7 1.8 %collective-permute-start = (bf16[8,1152]{1,0:T(8,128)(2,1)S(1)}, bf16[8,1152]{1,0:T(8,128)(2,1)S(1)}, u32[]{:S(2)}, u32[]{:S(2)}) collective-permute-start(bf16[8,1152]{1,0:T(8,128)(2,1)S(1)} %get-tuple-element.13), channel_id=1, source_target_pairs={{0,1},{1,0},{2,3},{3,2},{4,5},{5,4},{6,7},{7,6},{8,9},{9,8},{10,11... | collective-permute-start | bytes 55304 | tf_op jit(solution)/shard_map/ppermute | solution.py:71
  3.5 1.4 %collective-permute-start.1 = (bf16[8,1152]{1,0:T(8,128)(2,1)S(1)}, bf16[8,1152]{1,0:T(8,128)(2,1)S(1)}, u32[]{:S(2)}, u32[]{:S(2)}) collective-permute-start(bf16[8,1152]{1,0:T(8,128)(2,1)S(1)} %get-tuple-element.14), channel_id=1, source_target_pairs={{0,17},{1,16},{2,19},{3,18},{4,21},{5,20},{6,23},{7,22},{8,25},{9,... | collective-permute-start | bytes 55304 | tf_op jit(solution)/shard_map/ppermute | solution.py:71
  4.9 0.4 %collective-permute-start.2 = (bf16[8,1152]{1,0:T(8,128)(2,1)S(1)}, bf16[8,1152]{1,0:T(8,128)(2,1)S(1)}, u32[]{:S(2)}, u32[]{:S(2)}) collective-permute-start(bf16[8,1152]{1,0:T(8,128)(2,1)S(1)} %get-tuple-element.15), channel_id=1, source_target_pairs={{0,16},{1,17},{2,18},{3,19},{4,20},{5,21},{6,22},{7,23},{8,24},{9,... | collective-permute-start | bytes 55304 | tf_op jit(solution)/shard_map/ppermute | solution.py:71
  5.3 0.3 collective-permute-done.a1
  5.6 2.6 %collective-permute-done.1.a2 = bf16[8,1152]{1,0:T(8,128)(2,1)S(1)} collective-permute-done((bf16[8,1152]{1,0:T(8,128)(2,1)S(1)}, bf16[8,1152]{1,0:T(8,128)(2,1)S(1)}, u32[]{:S(2)}, u32[]{:S(2)}) %collective-permute-start.1) | collective-permute-done | bytes 18464 | tf_op jit(solution)/shard_map/ppermute | solution.py:71
  8.1 0.5 %collective-permute-done.2.a3 = bf16[8,1152]{1,0:T(8,128)(2,1)S(1)} collective-permute-done((bf16[8,1152]{1,0:T(8,128)(2,1)S(1)}, bf16[8,1152]{1,0:T(8,128)(2,1)S(1)}, u32[]{:S(2)}, u32[]{:S(2)}) %collective-permute-start.2) | collective-permute-done | bytes 18464 | tf_op jit(solution)/shard_map/ppermute | solution.py:71
  8.6 3.0 %collective-permute-start.6 = (bf16[32,384]{1,0:T(8,128)(2,1)S(1)}, bf16[32,384]{1,0:T(8,128)(2,1)S(1)}, u32[]{:S(2)}, u32[]{:S(2)}) collective-permute-start(bf16[32,384]{1,0:T(8,128)(2,1)S(1)} %get-tuple-element.17.a), channel_id=1, source_target_pairs={{0,3},{1,2},{2,1},{3,0},{4,7},{5,6},{6,5},{7,4},{8,11},{9,10},{10,... | collective-permute-start | bytes 73736 | tf_op jit(solution)/shard_map/ppermute | solution.py:71
  11.6 2.1 %collective-permute-start.5 = (bf16[32,768]{1,0:T(8,128)(2,1)S(1)}, bf16[32,768]{1,0:T(8,128)(2,1)S(1)}, u32[]{:S(2)}, u32[]{:S(2)}) collective-permute-start(bf16[32,768]{1,0:T(8,128)(2,1)S(1)} %get-tuple-element.16.kv0), channel_id=1, source_target_pairs={{0,48},{1,49},{2,50},{3,51},{4,52},{5,53},{6,54},{7,55},{8,56},{9,... | collective-permute-start | bytes 147464 | tf_op jit(solution)/shard_map/ppermute | solution.py:71
  13.7 4.0 %collective-permute-start.4 = (bf16[32,768]{1,0:T(8,128)(2,1)S(1)}, bf16[32,768]{1,0:T(8,128)(2,1)S(1)}, u32[]{:S(2)}, u32[]{:S(2)}) collective-permute-start(bf16[32,768]{1,0:T(8,128)(2,1)S(1)} %get-tuple-element.16.kv0), channel_id=1, source_target_pairs={{0,12},{1,13},{2,14},{3,15},{4,8},{5,9},{6,10},{7,11},{8,4},{9,5},... | collective-permute-start | bytes 147464 | tf_op jit(solution)/shard_map/ppermute | solution.py:71
  17.8 0.6 %collective-permute-start.3 = (bf16[32,768]{1,0:T(8,128)(2,1)S(1)}, bf16[32,768]{1,0:T(8,128)(2,1)S(1)}, u32[]{:S(2)}, u32[]{:S(2)}) collective-permute-start(bf16[32,768]{1,0:T(8,128)(2,1)S(1)} %get-tuple-element.16.kv0), channel_id=1, source_target_pairs={{0,60},{1,61},{2,62},{3,63},{4,56},{5,57},{6,58},{7,59},{8,52},{9,... | collective-permute-start | bytes 147464 | tf_op jit(solution)/shard_map/ppermute | solution.py:71
  18.4 0.0 collective-permute-done.6.b
  18.4 0.1 collective-permute-start.7
  19.1 1.4 %text.1 = (bf16[128,384]{1,0:T(8,128)(2,1)S(1)}, bf16[128,384]{1,0:T(8,128)(2,1)S(1)}, bf16[128,384]{1,0:T(8,128)(2,1)S(1)}, f32[8,128]{1,0:T(8,128)S(1)}) custom-call(bf16[512,1536]{1,0:T(8,128)(2,1)} %q_h.1, bf16[512,1536]{1,0:T(8,128)(2,1)} %k_h.1, bf16[512,1536]{1,0:T(8,128)(2,1)} %v_h.1, f32[1,128]{1,0:T(1,128)} %bitcast.6, f32[1,128]{1,0:T(1,128)} %bitcast.7, ...), custom_call_target="tpu_custom_call" | custom-call | flops 20000000 | bytes 600000 | tf_op jit(solution)/shard_map/text/pallas_call | solution.py:80
  20.5 0.0 collective-permute-done.5.kv3
  20.5 0.0 collective-permute-done.4.kv2
  20.5 4.7 %collective-permute-done.3.kv1 = bf16[32,768]{1,0:T(8,128)(2,1)S(1)} collective-permute-done((bf16[32,768]{1,0:T(8,128)(2,1)S(1)}, bf16[32,768]{1,0:T(8,128)(2,1)S(1)}, u32[]{:S(2)}, u32[]{:S(2)}) %collective-permute-start.3) | collective-permute-done | bytes 49184 | tf_op jit(solution)/shard_map/ppermute | solution.py:71
  25.2 0.0 collective-permute-done.7.q1
  25.2 0.8 %attend.1 = bf16[16,8,896]{2,1,0:T(8,128)(2,1)S(1)} custom-call(bf16[32,768]{1,0:T(8,128)(2,1)S(1)} %get-tuple-element.16.kv0, bf16[32,768]{1,0:T(8,128)(2,1)S(1)} %collective-permute-done.3.kv1, bf16[32,768]{1,0:T(8,128)(2,1)S(1)} %collective-permute-done.4.kv2, bf16[32,768]{1,0:T(8,128)(2,1)S(1)} %collective-permute-done.5.kv3, ...), custom_call_target="tpu_custom_call" | custom-call | tf_op jit(solution)/shard_map/attend/pallas_call | solution.py:375
  26.0 9.4 %all_to_all.5.got = bf16[16,8,896]{2,1,0:T(8,128)(2,1)S(1)} all-to-all(bf16[16,8,896]{2,1,0:T(8,128)(2,1)S(1)} %attend.1), channel_id=1, replica_groups={{16,0,17,1,18,2,19,3,20,4,21,5,22,6,23,7},{28,12,29,13,30,14,31,15,24,8..., dimensions={0} | all-to-all | bytes 458752 | tf_op jit(solution)/shard_map/all_to_all | solution.py:383
  35.3 0.9 %combine.1 = (bf16[8,1536]{1,0:T(8,128)(2,1)}, bf16[8,1536]{1,0:T(8,128)(2,1)}) custom-call(bf16[16,8,896]{2,1,0:T(8,128)(2,1)S(1)} %all_to_all.5.got), custom_call_target="tpu_custom_call" | custom-call | tf_op jit(solution)/shard_map/combine/pallas_call | solution.py:386
  (2 shorter events, 0.0 us)
Async XLA Ops:
  1.7 3.8 %collective-permute-start = (bf16[8,1152]{1,0:T(8,128)(2,1)S(1)}, bf16[8,1152]{1,0:T(8,128)(2,1)S(1)}, u32[]{:S(2)}, u32[]{:S(2)}) collective-permute-start(bf16[8,1152]{1,0:T(8,128)(2,1)S(1)} %get-tuple-element.13), channel_id=1, source_target_pairs={{0,1},{1,0},{2,3},{3,2},{4,5},{5,4},{6,7},{7,6},{8,9},{9,8},{10,11... | collective-permute-start | bytes 55304 | tf_op jit(solution)/shard_map/ppermute | solution.py:71
  3.5 4.7 %collective-permute-start.1 = (bf16[8,1152]{1,0:T(8,128)(2,1)S(1)}, bf16[8,1152]{1,0:T(8,128)(2,1)S(1)}, u32[]{:S(2)}, u32[]{:S(2)}) collective-permute-start(bf16[8,1152]{1,0:T(8,128)(2,1)S(1)} %get-tuple-element.14), channel_id=1, source_target_pairs={{0,17},{1,16},{2,19},{3,18},{4,21},{5,20},{6,23},{7,22},{8,25},{9,... | collective-permute-start | bytes 55304 | tf_op jit(solution)/shard_map/ppermute | solution.py:71
  4.9 3.8 %collective-permute-start.2 = (bf16[8,1152]{1,0:T(8,128)(2,1)S(1)}, bf16[8,1152]{1,0:T(8,128)(2,1)S(1)}, u32[]{:S(2)}, u32[]{:S(2)}) collective-permute-start(bf16[8,1152]{1,0:T(8,128)(2,1)S(1)} %get-tuple-element.15), channel_id=1, source_target_pairs={{0,16},{1,17},{2,18},{3,19},{4,20},{5,21},{6,22},{7,23},{8,24},{9,... | collective-permute-start | bytes 55304 | tf_op jit(solution)/shard_map/ppermute | solution.py:71
  8.6 9.7 %collective-permute-start.6 = (bf16[32,384]{1,0:T(8,128)(2,1)S(1)}, bf16[32,384]{1,0:T(8,128)(2,1)S(1)}, u32[]{:S(2)}, u32[]{:S(2)}) collective-permute-start(bf16[32,384]{1,0:T(8,128)(2,1)S(1)} %get-tuple-element.17.a), channel_id=1, source_target_pairs={{0,3},{1,2},{2,1},{3,0},{4,7},{5,6},{6,5},{7,4},{8,11},{9,10},{10,... | collective-permute-start | bytes 73736 | tf_op jit(solution)/shard_map/ppermute | solution.py:71
  11.6 8.9 %collective-permute-start.5 = (bf16[32,768]{1,0:T(8,128)(2,1)S(1)}, bf16[32,768]{1,0:T(8,128)(2,1)S(1)}, u32[]{:S(2)}, u32[]{:S(2)}) collective-permute-start(bf16[32,768]{1,0:T(8,128)(2,1)S(1)} %get-tuple-element.16.kv0), channel_id=1, source_target_pairs={{0,48},{1,49},{2,50},{3,51},{4,52},{5,53},{6,54},{7,55},{8,56},{9,... | collective-permute-start | bytes 147464 | tf_op jit(solution)/shard_map/ppermute | solution.py:71
  13.7 6.8 %collective-permute-start.4 = (bf16[32,768]{1,0:T(8,128)(2,1)S(1)}, bf16[32,768]{1,0:T(8,128)(2,1)S(1)}, u32[]{:S(2)}, u32[]{:S(2)}) collective-permute-start(bf16[32,768]{1,0:T(8,128)(2,1)S(1)} %get-tuple-element.16.kv0), channel_id=1, source_target_pairs={{0,12},{1,13},{2,14},{3,15},{4,8},{5,9},{6,10},{7,11},{8,4},{9,5},... | collective-permute-start | bytes 147464 | tf_op jit(solution)/shard_map/ppermute | solution.py:71
  17.8 7.4 %collective-permute-start.3 = (bf16[32,768]{1,0:T(8,128)(2,1)S(1)}, bf16[32,768]{1,0:T(8,128)(2,1)S(1)}, u32[]{:S(2)}, u32[]{:S(2)}) collective-permute-start(bf16[32,768]{1,0:T(8,128)(2,1)S(1)} %get-tuple-element.16.kv0), channel_id=1, source_target_pairs={{0,60},{1,61},{2,62},{3,63},{4,56},{5,57},{6,58},{7,59},{8,52},{9,... | collective-permute-start | bytes 147464 | tf_op jit(solution)/shard_map/ppermute | solution.py:71
  18.4 6.8 %collective-permute-start.7 = (bf16[64,384]{1,0:T(8,128)(2,1)S(1)}, bf16[64,384]{1,0:T(8,128)(2,1)S(1)}, u32[]{:S(2)}, u32[]{:S(2)}) collective-permute-start(bf16[64,384]{1,0:T(8,128)(2,1)S(1)} %join.1.q0), channel_id=1, source_target_pairs={{0,4},{1,5},{2,6},{3,7},{4,0},{5,1},{6,2},{7,3},{8,12},{9,13},{10,... | collective-permute-start | bytes 147464 | tf_op jit(solution)/shard_map/ppermute | solution.py:71
